TPU v7x, 32 devices: a whole 2x2x4 slice. The times are simulated.
32 devices in a mesh: aux: 4 (over z), orb: 8 (over y, x, core).
Axes of the slice: x: 2, y: 2, z: 4, core: 2. Of those that a mesh axis runs over, the one named last changes fastest.
Arguments:
- half: bfloat16 [64, 384, 3072], P('aux', 'orb'), may hold values from -1.25 to 1.25
- metric: bfloat16 [64, 64], P('aux'), may hold values from -1 to 2
- survive: int32 [4, 16, 24], P('aux', 'orb'), may hold values 0 or 1
Outputs:
- exchange_k: float32 [3072, 3072], P('orb', 'aux')
All inputs are finite; a program needn't handle non-finite values. No bound on the sum of `survive` on one device may be relied on, other than what follows from the above.
Results may differ from a plain program's by a relative error of at most 0.00098.
Values may be sent and summed in bfloat16 or wider, within the bound.
A program may use at most 128 MiB of HBM per device.

v0:
```python
import jax
import jax.numpy as jnp
from jax import lax
from jax.sharding import PartitionSpec as P


def shards(half, metric, survive):
    aux_local, occ_local, ao_count = half.shape
    blocks_aux, blocks_occ, blocks_ao = survive.shape
    gate = survive.astype(jnp.bfloat16)
    shaped = half.reshape(
        blocks_aux, aux_local, blocks_occ, occ_local // blocks_occ, blocks_ao, ao_count // blocks_ao
    )
    masked = (shaped * gate[:, None, :, None, :, None]).reshape(aux_local, occ_local, ao_count)
    portion = lax.all_gather(masked, "aux", axis=0, tiled=True)
    fit_total = jnp.dot(
        metric, portion.reshape(portion.shape[0], -1), preferred_element_type=jnp.float32
    )
    fitted = fit_total.astype(jnp.bfloat16).reshape(aux_local, occ_local, ao_count)
    group_width = ao_count // lax.axis_size("orb")
    row_start = lax.axis_index("orb") * group_width
    flat_rows = lax.all_gather(fitted, "orb", axis=1, tiled=True).reshape(-1, ao_count)
    left_rows = lax.dynamic_slice_in_dim(flat_rows, row_start, group_width, 1)
    partial_k = lax.dot_general(
        left_rows, flat_rows, (((0,), (0,)), ((), ())), preferred_element_type=jnp.float32
    )
    return lax.psum_scatter(partial_k, "aux", scatter_dimension=1, tiled=True)


def solution(mesh):
    return jax.shard_map(
        shards,
        mesh=mesh,
        in_specs=(P("aux", "orb", None), P("aux", None), P("aux", "orb", None)),
        out_specs=P("orb", "aux"),
        check_vma=False,
    )
```

profile of v0, /device:TPU:0, one launch (start us, length us, event | category | flops | bytes accessed | tf_op | source)
XLA Modules:
  0.0 656.1 jit_solution(17843219238067424248)
XLA Ops:
  6.5 0.0 copy-start
  6.5 0.0 all-gather.3.cloned.1.call-start
  6.5 0.7 convert_bitcast_fusion
  7.2 0.1 mul.21
  7.4 5.1 broadcast_multiply_fusion
  12.5 0.0 all-gather.3.cloned.1.call-update
  12.5 0.0 all-gather.5.cloned.1.call-start
  12.6 325.4 %all-gather.3.cloned.1.call-done = bf16[64,48,3072]{2,1,0:T(8,128)(2,1)} async-done(((bf16[16,48,3072]{2,1,0:T(8,128)(2,1)}), bf16[64,48,3072]{2,1,0:T(8,128)(2,1)}) %all-gather.3.cloned.1.call-update) | async-done | bytes 18874384 | tf_op jit(solution)/shard_map/all_gather | solution.py:15
  338.0 17.5 %copy.5 = bf16[8,8,48,3072]{3,1,2,0:T(8,128)(2,1)S(1)} copy(bf16[8,8,48,3072]{3,2,1,0:T(8,128)(2,1)} %bitcast.18) | data formatting | bytes 37748736
  355.5 0.0 copy-done
  355.5 2.7 convolution_convert_fusion
  358.3 4.7 copy.6
  363.0 0.0 all-gather.5.cloned.1.call-update
  363.0 0.0 reduce-scatter.2.cloned.1.call-start
  363.1 178.4 %all-gather.5.cloned.1.call-done = bf16[16,384,3072]{2,1,0:T(8,128)(2,1)} async-done(((bf16[16,48,3072]{2,1,0:T(8,128)(2,1)}), bf16[16,384,3072]{2,1,0:T(8,128)(2,1)}) %all-gather.5.cloned.1.call-update) | async-done | bytes 37748752 | tf_op jit(solution)/shard_map/all_gather | solution.py:22
  541.5 0.0 copy-start.1
  541.5 22.4 %fusion = f32[384,3072]{1,0:T(8,128)} fusion(bf16[6144,3072]{1,0:T(8,128)(2,1)} %bitcast.22, s32[]{:T(128)S(6)} %select_n.3), kind=kOutput, calls=%fused_computation.1 | convolution fusion | flops 14495514624 | bytes 47185924 | tf_op jit(solution)/shard_map/dot_general | solution.py:24
  563.9 0.0 reduce-scatter.2.cloned.1.call-update
  563.9 85.6 %reduce-scatter.2.cloned.1.call-done = f32[384,768]{1,0:T(8,128)} async-done(((f32[384,3072]{1,0:T(8,128)}), f32[384,768]{1,0:T(8,128)}) %reduce-scatter.2.cloned.1.call-update) | async-done | bytes 1179664 | tf_op jit(solution)/shard_map/reduce_scatter | solution.py:27
  649.5 0.0 copy-done.1
  (1 shorter events, 0.0 us)
Async XLA Ops:
  6.5 349.0 %copy-start = (bf16[16,64]{1,0:T(8,128)(2,1)S(1)}, bf16[16,64]{1,0:T(8,128)(2,1)}, u32[]{:S(2)}) copy-start(bf16[16,64]{1,0:T(8,128)(2,1)} %param.4) | copy-start | bytes 6148
  6.5 331.5 %all-gather.3.cloned.1.call-start = ((), (), s32[]{:S(2)}) async-start(), calls=%async_computation.1 | async-start | bytes 23592960 | tf_op jit(solution)/shard_map/all_gather | solution.py:15
  12.5 528.9 %all-gather.5.cloned.1.call-start = ((), (), s32[]{:S(2)}) async-start(), calls=%async_computation.2 | async-start | bytes 42467328 | tf_op jit(solution)/shard_map/all_gather | solution.py:22
  363.0 286.5 %reduce-scatter.2.cloned.1.call-start = ((), (), s32[]{:S(2)}) async-start(), calls=%async_computation.3 | async-start | bytes 5898240 | tf_op jit(solution)/shard_map/reduce_scatter | solution.py:27
  541.5 108.1 %copy-start.1 = (bf16[16,64]{1,0:T(8,128)(2,1)S(1)}, bf16[16,64]{1,0:T(8,128)(2,1)}, u32[]{:S(2)}) copy-start(bf16[16,64]{1,0:T(8,128)(2,1)} %param.4) | copy-start | bytes 6148
Sparse Core Ops, SparseCore 0:
  12.7 325.2 all-gather.2
  363.2 178.2 all-gather.4
  564.0 85.4 reduce-scatter.1
where the time goes:
time: 656 us
  waiting for transfers between devices  589 us (90%)
  matrix products  25.2 us (4%)
  local copies, waits for them, and re-layouts  22.4 us (3%)
  between operations  13.2 us (2%)
    all_gather x1, waiting for transfers between devices, shards(): portion = lax.all_gather(masked, 'aux', axis=0, tiled=True)  325 us
    all_gather x1, waiting for transfers between devices, shards(): lax.all_gather(fitted, 'orb', axis=1, tiled=True).reshape(-1, ao_count)  178 us
    reduce_scatter x1, waiting for transfers between devices, shards(): return lax.psum_scatter(partial_k, 'aux', scatter_dimension=1, tiled=True)  85.6 us
    dot_general x1, matrix products, shards(): lax.dot_general(left_rows, flat_rows, (((0,), (0,)), ((), ())), preferred...  22.4 us
    unnamed x7, local copies, waits for them, and re-layouts  22.3 us
  transfers between devices with their start and end apart: 3, of which 3 were waited for; matrix products, arithmetic and copies ran while one was open for 0% of the time, Pallas kernels for 0%

commit v1 on v0

--- a/solution.py
+++ b/solution.py
@@ -12,7 +12,12 @@
         blocks_aux, aux_local, blocks_occ, occ_local // blocks_occ, blocks_ao, ao_count // blocks_ao
     )
     masked = (shaped * gate[:, None, :, None, :, None]).reshape(aux_local, occ_local, ao_count)
-    portion = lax.all_gather(masked, "aux", axis=0, tiled=True)
+    ring = [masked]
+    for hop in range(3):
+        ring.append(lax.ppermute(ring[-1], "aux", [(dev, (dev + 1) % 4) for dev in range(4)]))
+    portion = jnp.roll(
+        jnp.concatenate(ring[::-1], axis=0), (lax.axis_index("aux") + 1) * ring[0].shape[0], axis=0
+    )
     fit_total = jnp.dot(
         metric, portion.reshape(portion.shape[0], -1), preferred_element_type=jnp.float32
     )

time: 656 us -> 709 us (1.081)
  local copies, waits for them, and re-layouts: 22.4 us -> 80.3 us
  waiting for transfers between devices: 589 us -> 576 us
    all_gather x1 -> x0, waiting for transfers between devices: 325 us -> none  [shards(): portion = lax.all_gather(masked, 'aux', axis=0, tiled=True)]
    ppermute x0 -> x3, waiting for transfers between devices: none -> 313 us  [shards(): lax.ppermute(ring[-1], 'aux', [(dev, (dev + 1) % 4) for dev in range(4)])]
    unnamed x7 -> x21, local copies, waits for them, and re-layouts: 22.3 us -> 70.7 us
    dynamic_slice x0 -> x1, local copies, waits for them, and re-layouts: none -> 9.46 us  [shards(): jnp.roll(jnp.concatenate(ring[::-1], axis=0), (lax.axis_index('aux') + 1)...]
  transfers between devices with their start and end apart: 3 -> 5, of which waited for: 3 -> 5; matrix products, arithmetic and copies ran while one was open for 0% -> 0% of each run, Pallas kernels for 0% -> 0%
where the time goes in v1:
time: 709 us
  waiting for transfers between devices  576 us (81%)
  local copies, waits for them, and re-layouts  80.3 us (11%)
  matrix products  25.2 us (4%)
  between operations  13.5 us (2%)
  other arithmetic  10.7 us (2%)
    ppermute x3, waiting for transfers between devices, shards(): lax.ppermute(ring[-1], 'aux', [(dev, (dev + 1) % 4) for dev in range(4)])  313 us
    all_gather x1, waiting for transfers between devices, shards(): lax.all_gather(fitted, 'orb', axis=1, tiled=True).reshape(-1, ao_count)  177 us
    reduce_scatter x1, waiting for transfers between devices, shards(): return lax.psum_scatter(partial_k, 'aux', scatter_dimension=1, tiled=True)  85.6 us
    unnamed x21, local copies, waits for them, and re-layouts  70.7 us
    dot_general x1, matrix products, shards(): lax.dot_general(left_rows, flat_rows, (((0,), (0,)), ((), ())), preferred...  22.4 us
  transfers between devices with their start and end apart: 5, of which 5 were waited for; matrix products, arithmetic and copies ran while one was open for 0% of the time, Pallas kernels for 0%

profile of v1, /device:TPU:0, one launch (start us, length us, event | category | flops | bytes accessed | tf_op | source)
XLA Modules:
  0.0 708.7 jit_solution(3638923824115434351)
XLA Ops:
  6.5 0.0 copy-start
  6.5 0.0 all-gather.2.cloned.1.call-start
  6.5 0.7 convert_bitcast_fusion
  7.2 0.1 mul.24
  7.4 0.0 slice-start
  7.4 3.0 broadcast_multiply_fusion
  10.4 3.1 collective-permute-start
  13.5 103.8 %collective-permute-done = bf16[16,48,3072]{2,1,0:T(8,128)(2,1)S(1)} collective-permute-done((bf16[16,48,3072]{2,1,0:T(8,128)(2,1)S(1)}, bf16[16,48,3072]{2,1,0:T(8,128)(2,1)S(1)}, u32[]{:S(2)}, u32[]{:S(2)}) %collective-permute-start) | collective-permute-done | bytes 4718624 | tf_op jit(solution)/shard_map/ppermute | solution.py:17
  117.4 0.0 copy-start.1
  117.4 2.1 copy-done.1
  119.4 0.0 collective-permute-start.1
  119.4 104.9 %collective-permute-done.1 = bf16[16,48,3072]{2,1,0:T(8,128)(2,1)} collective-permute-done((bf16[16,48,3072]{2,1,0:T(8,128)(2,1)S(1)}, bf16[16,48,3072]{2,1,0:T(8,128)(2,1)}, u32[]{:S(2)}, u32[]{:S(2)}) %collective-permute-start.1) | collective-permute-done | bytes 4718624 | tf_op jit(solution)/shard_map/ppermute | solution.py:17
  224.3 0.0 collective-permute-start.2
  224.3 0.0 slice-start.2
  224.3 0.0 slice-start.1
  224.3 104.2 %collective-permute-done.2 = bf16[16,48,3072]{2,1,0:T(8,128)(2,1)} collective-permute-done((bf16[16,48,3072]{2,1,0:T(8,128)(2,1)}, bf16[16,48,3072]{2,1,0:T(8,128)(2,1)}, u32[]{:S(2)}, u32[]{:S(2)}) %collective-permute-start.2) | collective-permute-done | bytes 4718624 | tf_op jit(solution)/shard_map/ppermute | solution.py:17
  328.6 4.9 constant_dynamic-update-slice_fusion.7
  333.5 0.0 slice-start.3
  333.5 5.0 constant_dynamic-update-slice_fusion.6
  338.5 0.0 slice-done.2
  338.5 0.0 slice-done.3
  338.5 2.7 constant_dynamic-update-slice_fusion.5
  341.2 0.0 slice-done
  341.2 0.0 slice-done.1
  341.2 3.5 constant_dynamic-update-slice_fusion.4
  344.6 5.0 constant_dynamic-update-slice_fusion.3
  349.6 5.0 constant_dynamic-update-slice_fusion.2
  354.6 2.6 constant_dynamic-update-slice_fusion.1
  357.2 3.6 constant_dynamic-update-slice_fusion
  360.7 9.5 %constant_dynamic-slice_fusion = bf16[64,48,3072]{2,1,0:T(8,128)(2,1)S(1)} fusion(bf16[128,48,3072]{2,1,0:T(8,128)(2,1)} %constant_dynamic-update-slice_fusion, s32[]{:T(128)S(6)} %select_n.17), kind=kLoop, calls=%fused_computation.14 | loop fusion | bytes 37748740 | tf_op jit(solution)/shard_map/jit(_roll_dynamic)/dynamic_slice | solution.py:18
  370.2 38.7 %copy.5 = bf16[8,8,48,3072]{3,1,2,0:T(8,128)(2,1)S(1)} copy(bf16[8,8,48,3072]{3,2,1,0:T(8,128)(2,1)S(1)} %bitcast.17) | data formatting | bytes 37748736
  408.9 0.0 copy-done
  408.9 2.7 convolution_convert_fusion
  411.7 4.7 copy.6
  416.4 0.0 all-gather.2.cloned.1.call-update
  416.4 0.2 reduce-scatter.2.cloned.1.call-start
  416.6 177.1 %all-gather.2.cloned.1.call-done = bf16[16,384,3072]{2,1,0:T(8,128)(2,1)} async-done(((bf16[16,48,3072]{2,1,0:T(8,128)(2,1)}), bf16[16,384,3072]{2,1,0:T(8,128)(2,1)}) %all-gather.2.cloned.1.call-update) | async-done | bytes 37748752 | tf_op jit(solution)/shard_map/all_gather | solution.py:27
  593.8 22.4 %fusion = f32[384,3072]{1,0:T(8,128)} fusion(bf16[6144,3072]{1,0:T(8,128)(2,1)} %bitcast.28, s32[]{:T(128)S(6)} %select_n.18), kind=kOutput, calls=%fused_computation.1 | convolution fusion | flops 14495514624 | bytes 47185924 | tf_op jit(solution)/shard_map/dot_general | solution.py:29
  616.2 0.0 reduce-scatter.2.cloned.1.call-update
  616.2 85.6 %reduce-scatter.2.cloned.1.call-done = f32[384,768]{1,0:T(8,128)} async-done(((f32[384,3072]{1,0:T(8,128)}), f32[384,768]{1,0:T(8,128)}) %reduce-scatter.2.cloned.1.call-update) | async-done | bytes 1179664 | tf_op jit(solution)/shard_map/reduce_scatter | solution.py:32
  (3 shorter events, 0.0 us)
Async XLA Ops:
  6.5 402.4 %copy-start = (bf16[16,64]{1,0:T(8,128)(2,1)S(1)}, bf16[16,64]{1,0:T(8,128)(2,1)}, u32[]{:S(2)}) copy-start(bf16[16,64]{1,0:T(8,128)(2,1)} %param.4) | copy-start | bytes 6148
  6.5 587.2 %all-gather.2.cloned.1.call-start = ((), (), s32[]{:S(2)}) async-start(), calls=%async_computation.1 | async-start | bytes 42467328 | tf_op jit(solution)/shard_map/all_gather | solution.py:27
  7.4 333.8 %slice-start = ((s8[4718592]{0:T(1024)(128)(4,1)}), s8[524288]{0:T(1024)(128)(4,1)S(1)}, s32[]{:S(2)}) async-start(s8[4718592]{0:T(1024)(128)(4,1)} %bitcast.18), calls=%async_computation.3 | async-start | bytes 1048576
  10.4 106.9 %collective-permute-start = (bf16[16,48,3072]{2,1,0:T(8,128)(2,1)S(1)}, bf16[16,48,3072]{2,1,0:T(8,128)(2,1)S(1)}, u32[]{:S(2)}, u32[]{:S(2)}) collective-permute-start(bf16[16,48,3072]{2,1,0:T(8,128)(2,1)S(1)} %broadcast_multiply_fusion), channel_id=1, source_target_pairs={{0,8},{8,16},{16,24},{24,0},{1,9},{9,17},{17,25},{25,1},{2,10},{10... | collective-permute-start | bytes 14155784 | tf_op jit(solution)/shard_map/ppermute | solution.py:17
  117.4 2.1 copy-start.1
  119.4 104.9 %collective-permute-start.1 = (bf16[16,48,3072]{2,1,0:T(8,128)(2,1)S(1)}, bf16[16,48,3072]{2,1,0:T(8,128)(2,1)}, u32[]{:S(2)}, u32[]{:S(2)}) collective-permute-start(bf16[16,48,3072]{2,1,0:T(8,128)(2,1)S(1)} %collective-permute-done), channel_id=1, source_target_pairs={{0,8},{8,16},{16,24},{24,0},{1,9},{9,17},{17,25},{25,1},{2,10},{10... | collective-permute-start | bytes 14155784 | tf_op jit(solution)/shard_map/ppermute | solution.py:17
  224.3 104.2 %collective-permute-start.2 = (bf16[16,48,3072]{2,1,0:T(8,128)(2,1)}, bf16[16,48,3072]{2,1,0:T(8,128)(2,1)}, u32[]{:S(2)}, u32[]{:S(2)}) collective-permute-start(bf16[16,48,3072]{2,1,0:T(8,128)(2,1)} %collective-permute-done.1), channel_id=1, source_target_pairs={{0,8},{8,16},{16,24},{24,0},{1,9},{9,17},{17,25},{25,1},{2,10},{10... | collective-permute-start | bytes 14155784 | tf_op jit(solution)/shard_map/ppermute | solution.py:17
  224.3 114.2 %slice-start.2 = ((s8[4718592]{0:T(1024)(128)(4,1)}), s8[4194304]{0:T(1024)(128)(4,1)S(1)}, s32[]{:S(2)}) async-start(s8[4718592]{0:T(1024)(128)(4,1)} %bitcast.21), calls=%async_computation.5 | async-start | bytes 8388608
  224.3 116.8 %slice-start.1 = ((s8[4718592]{0:T(1024)(128)(4,1)}), s8[4194304]{0:T(1024)(128)(4,1)S(1)}, s32[]{:S(2)}) async-start(s8[4718592]{0:T(1024)(128)(4,1)} %bitcast.18), calls=%async_computation.4 | async-start | bytes 8388608
  333.5 5.0 slice-start.3
  416.4 285.4 %reduce-scatter.2.cloned.1.call-start = ((), (), s32[]{:S(2)}) async-start(), calls=%async_computation.2 | async-start | bytes 5898240 | tf_op jit(solution)/shard_map/reduce_scatter | solution.py:32
Sparse Core Ops, SparseCore 0:
  416.5 177.1 all-gather.1
  616.4 85.4 reduce-scatter.1
